TPU v7x, 256 devices: a whole 4x4x8 slice. The times are simulated.
256 devices in a mesh: grp: 8 (over y_hi, x), dev: 32 (over z, y_lo, core).
Axes of the slice: x: 4, y: 4 (y_hi: 2, y_lo: 2; y = y_hi * 2 + y_lo), z: 8, core: 2. Of those that a mesh axis runs over, the one named last changes fastest.
Arguments:
- queries: bfloat16 [32768, 256], P(('grp', 'dev')), may hold values from -32 to 32
- items: bfloat16 [32768, 256], P(('grp', 'dev')), may hold values from -24 to 24
- item_ids: int32 [32768], P('grp'), may hold values from 0 to 262143
- neg_embed: bfloat16 [16384, 256], P('dev'), may hold values from -6 to 6
- neg_logq: float32 [16384], P('dev'), may hold values from -12 to -8
- logq_table: float32 [262144], replicated, may hold values from -11 to -9.5
Outputs:
- query_loss: float32 [32768], P(('grp', 'dev'))
- query_grad: float32 [32768, 256], P(('grp', 'dev'))
- item_grad: float32 [32768, 256], P(('grp', 'dev'))
- negative_grad: float32 [16384, 256], P('dev')
Inputs may be any that keep to these rules, and one draw needn't show every extreme that they name: `item_ids`: a row of logq_table.
All inputs are finite; a program needn't handle non-finite values.
Results may differ from a plain program's by a relative error of at most 0.0036.
Values may be sent and summed in bfloat16 or wider, within the bound.
A program may use at most 64 MiB of HBM per device.

v0:
```python
import jax
import jax.numpy as jnp
from jax import lax
from jax.sharding import PartitionSpec as P

logit_scale = 0.25


def from_everyone(shard, axis):
    length = lax.axis_size(axis)
    return lax.all_to_all(
        jnp.broadcast_to(shard[None], (length, *shard.shape)), axis, 0, 0, tiled=True
    )


def all_in_one(shard, axis):
    leaves = jax.tree.leaves(shard)
    order = sorted(range(len(leaves)), key=lambda k: -leaves[k].size)
    width = (1, *leaves[order[0]].shape)[-1]
    lines = [
        jnp.pad(leaves[k].reshape(-1), (0, -leaves[k].size % width)).reshape(-1, width)
        for k in order
    ]
    both, at, found = (from_everyone(jnp.concatenate(lines), axis), 0, {})
    for k, line in zip(order, lines):
        section = both[:, at : at + len(line)].reshape(len(both), -1)
        found[k] = section[:, : leaves[k].size].reshape(-1, *leaves[k].shape)
        at += len(line)
    numbers = iter(range(len(leaves)))
    return jax.tree.map(lambda _: found[next(numbers)], shard)


def folded_in_pairs(pieces, combine):
    while len(jax.tree.leaves(pieces)[0]) > 1:
        pieces = jax.vmap(combine)(
            *(jax.tree.map(lambda part: part[side::2], pieces) for side in (0, 1))
        )
    return jax.tree.map(lambda part: part[0], pieces)


def joined_all(shard, axis, combine):
    pieces = all_in_one(shard, axis)
    return folded_in_pairs(pieces, combine)


def cut_along(shard, dim, length):
    before, after = (shard.shape[:dim], shard.shape[dim + 1 :])
    return jnp.moveaxis(shard.reshape(*before, length, -1, *after), dim, 0)


def summed_on_arrival(shard, axis, dim):
    pieces = cut_along(shard, dim, lax.axis_size(axis))
    arrived = lax.all_to_all(pieces, axis, split_axis=0, concat_axis=0, tiled=True)
    return arrived.astype(jnp.float32).sum(axis=0)


def taken_together(shard, axis):
    return from_everyone(shard, axis).sum(axis=0)


def block_shape(all_rows):
    block_rows = min(512, all_rows)
    return (block_rows, all_rows // block_rows)


def combine_stats(earlier, later):
    row_max = jnp.maximum(earlier[0], later[0])
    return (
        row_max,
        earlier[1] * jnp.exp(earlier[0] - row_max) + later[1] * jnp.exp(later[0] - row_max),
    )


def log_total(maxima, totals):
    row_max, row_sum = joined_all((maxima, totals), "dev", combine_stats)
    return row_max + jnp.log(row_sum)


def row_stats(scores):
    row_max = jnp.max(scores, axis=1)
    return (row_max, jnp.sum(jnp.exp(scores - row_max[:, None]), axis=1))


def logits(q_block, candidates, cand_offsets):
    return (
        logit_scale * jnp.dot(q_block, candidates.T, preferred_element_type=jnp.float32)
        - cand_offsets[None, :]
    )


def local(queries, items, item_ids, neg_embed, neg_logq, logq_table):
    own_rows, feat_width = queries.shape
    dev_index = lax.axis_index("dev")
    own_start = dev_index * own_rows
    own_ids = lax.dynamic_slice_in_dim(item_ids, own_start, own_rows, 0)
    own_offsets = jnp.take(logq_table, own_ids, axis=0)
    group_q = lax.all_gather(queries, "dev", axis=0, tiled=True)
    all_rows = group_q.shape[0]
    block_rows, block_count = block_shape(all_rows)
    blocks = group_q.reshape(block_count, block_rows, feat_width)
    starts = jnp.arange(block_count, dtype=jnp.int32) * block_rows
    candidates = jnp.concatenate([items, neg_embed], axis=0)
    cand_offsets = jnp.concatenate([own_offsets, neg_logq], axis=0)
    columns = jnp.arange(candidates.shape[0], dtype=jnp.int32)

    def positives(first_row):
        targets = first_row + jnp.arange(block_rows, dtype=jnp.int32) - own_start
        return (columns[None, :] == targets[:, None]) & (columns[None, :] < own_rows)

    def forward(packed):
        q_block, first_row = packed
        scores = logits(q_block, candidates, cand_offsets)
        row_max, row_sum = row_stats(scores)
        return (row_max, row_sum, jnp.sum(jnp.where(positives(first_row), scores, 0.0), axis=1))

    maxima, totals, matched = lax.map(forward, (blocks, starts))
    log_norm = log_total(maxima.reshape(all_rows), totals.reshape(all_rows))
    own_norm = lax.dynamic_slice_in_dim(log_norm, own_start, own_rows, 0)
    own_match = lax.dynamic_slice_in_dim(matched.reshape(all_rows), own_start, own_rows, 0)
    query_loss = own_norm - own_match

    def backward(summed, packed):
        q_block, first_row, block_norm = packed
        scores = logits(q_block, candidates, cand_offsets)
        logit_grad = (
            logit_scale
            * (jnp.exp(scores - block_norm[:, None]) - positives(first_row).astype(jnp.float32))
        ).astype(jnp.bfloat16)
        summed = summed + jnp.einsum(
            "rc,rd->cd", logit_grad, q_block, preferred_element_type=jnp.float32
        )
        return (summed, jnp.dot(logit_grad, candidates, preferred_element_type=jnp.float32))

    zero_acc = jnp.zeros((candidates.shape[0], feat_width), jnp.float32)
    cand_grad, q_partial = lax.scan(
        backward, zero_acc, (blocks, starts, log_norm.reshape(block_count, block_rows))
    )
    query_grad = summed_on_arrival(
        q_partial.reshape(all_rows, feat_width).astype(jnp.bfloat16), "dev", 0
    )
    item_grad = cand_grad[:own_rows]
    negative_part = cand_grad[own_rows:]
    negative_grad = taken_together(negative_part, "grp")
    return (query_loss, query_grad, item_grad, negative_grad)


def solution(mesh):
    return jax.shard_map(
        local,
        mesh=mesh,
        in_specs=(
            P(("grp", "dev"), None),
            P(("grp", "dev"), None),
            P("grp"),
            P("dev", None),
            P("dev"),
            P(),
        ),
        out_specs=(
            P(("grp", "dev")),
            P(("grp", "dev"), None),
            P(("grp", "dev"), None),
            P("dev", None),
        ),
        check_vma=False,
    )
```

profile of v0, /device:TPU:9, one launch (start us, length us, event | category | flops | bytes accessed | tf_op | source)
XLA Modules:
  0.0 316.9 jit_solution(15767919707973878997)
XLA Ops:
  13.2 63.8 %all-gather.2.cloned.1.call-done = bf16[4096,256]{1,0:T(8,128)(2,1)} async-done(((bf16[128,256]{1,0:T(8,128)(2,1)}), bf16[4096,256]{1,0:T(8,128)(2,1)}) %all-gather.2.cloned.1.call-update) | async-done | bytes 2097168 | tf_op jit(solution)/shard_map/all_gather | solution.py:97
  77.0 28.9 %while.30 = (s32[]{:T(128)}, f32[8,512]{1,0:T(8,128)S(1)}, f32[8,512]{1,0:T(8,128)S(1)}, f32[8,512]{1,0:T(8,128)S(1)}, bf16[8,512,256]{2,1,0:T(8,128)(2,1)}, /*i...) while((s32[]{:T(128)}, f32[8,512]{1,0:T(8,128)S(1)}, ...), condition=%wide.region_4.5_spmd.clone.clone, body=%wide.region_0.4_spmd.clone.clone.sunk | while | flops 170721408 | bytes 3239833 | solution.py:116
  107.4 7.4 %all-to-all-start = ((f32[32,2,4096]{2,1,0:T(2,128)}), f32[32,2,4096]{2,1,0:T(2,128)S(1)}, u32[]{:S(2)}, u32[]{:S(2)}) async-start(f32[32,2,4096]{2,1,0:T(2,128)} %broadcast_in_dim.56), calls=%async_computation | async-start | bytes 2097152 | tf_op jit(solution)/shard_map/all_to_all | solution.py:11
  114.8 28.3 %all-to-all-done = f32[32,2,4096]{2,1,0:T(2,128)S(1)} async-done(((f32[32,2,4096]{2,1,0:T(2,128)}), f32[32,2,4096]{2,1,0:T(2,128)S(1)}, u32[]{:S(2)}, u32[]{:S(2)}) %all-to-all-start) | async-done | bytes 1048608 | tf_op jit(solution)/shard_map/all_to_all | solution.py:11
  149.9 43.4 %while.31 = (s32[]{:T(128)}, f32[640,256]{1,0:T(8,128)S(1)}, bf16[8,512,256]{2,1,0:T(8,128)(2,1)}, bf16[8,512,256]{2,1,0:T(8,128)(2,1)}, bf16[640,256]{1,0:T(8,1...) while((s32[]{:T(128)}, f32[640,256]{1,0:T(8,128)S(1)}, ...), condition=%wide.region_6.7_spmd.clone.clone, body=%wide.region_5.6_spmd.clone.clone.sunk | while | flops 506594944 | bytes 4994979 | solution.py:135
  151.2 1.6 fusion.51
  152.8 1.5 convolution_add_fusion.2
  156.6 1.6 fusion.51
  162.1 1.6 fusion.51
  163.6 1.5 convolution_add_fusion.2
  167.5 1.6 fusion.51
  169.1 1.5 convolution_add_fusion.2
  172.9 1.6 fusion.51
  174.5 1.5 convolution_add_fusion.2
  178.3 1.6 fusion.51
  179.9 1.5 convolution_add_fusion.2
  183.7 1.6 fusion.51
  185.3 1.5 convolution_add_fusion.2
  189.1 1.6 fusion.51
  193.7 55.2 %all_to_all.15 = f32[8,512,256]{2,1,0:T(8,128)} all-to-all(f32[8,512,256]{2,1,0:T(8,128)S(1)} %broadcast_in_dim.59), channel_id=1, replica_groups=mesh['grp'=8,'dev'=32] {'grp'}, dimensions={0} | all-to-all | bytes 8388608 | tf_op jit(solution)/shard_map/all_to_all | solution.py:11
  248.9 7.1 %all-to-all-start.1 = ((bf16[32,128,256]{2,1,0:T(8,128)(2,1)}), bf16[32,128,256]{2,1,0:T(8,128)(2,1)}, u32[]{:S(2)}, u32[]{:S(2)}) async-start(bf16[32,128,256]{2,1,0:T(8,128)(2,1)} %bitcast.72), calls=%async_computation.1 | async-start | bytes 4194304 | tf_op jit(solution)/shard_map/all_to_all | solution.py:53
  257.3 3.3 %reduce_sum.37 = f32[512,256]{1,0:T(8,128)} reduce(f32[8,512,256]{2,1,0:T(8,128)} %all_to_all.15, f32[]{:T(128)} %constant.43.clone.1), dimensions={0}, to_apply=%region_8.9 | reduce | flops 917504 | bytes 4718596 | tf_op jit(solution)/shard_map/reduce_sum | solution.py:58
  260.6 47.0 %all-to-all-done.1 = bf16[32,128,256]{2,1,0:T(8,128)(2,1)} async-done(((bf16[32,128,256]{2,1,0:T(8,128)(2,1)}), bf16[32,128,256]{2,1,0:T(8,128)(2,1)}, u32[]{:S(2)}, u32[]{:S(2)}) %all-to-all-start.1) | async-done | bytes 2097184 | tf_op jit(solution)/shard_map/all_to_all | solution.py:53
  307.5 2.5 convert_reduce_fusion
  (157 shorter events, 66.0 us)
Async XLA Ops:
  7.2 1.6 copy-start
  7.2 69.8 %all-gather.2.cloned.1.call-start = ((), (), s32[]{:S(2)}) async-start(), calls=%async_computation.3 | async-start | bytes 2162688 | tf_op jit(solution)/shard_map/all_gather | solution.py:97
  107.4 35.6 %all-to-all-start = ((f32[32,2,4096]{2,1,0:T(2,128)}), f32[32,2,4096]{2,1,0:T(2,128)S(1)}, u32[]{:S(2)}, u32[]{:S(2)}) async-start(f32[32,2,4096]{2,1,0:T(2,128)} %broadcast_in_dim.56), calls=%async_computation | async-start | bytes 2097152 | tf_op jit(solution)/shard_map/all_to_all | solution.py:11
  248.9 58.6 %all-to-all-start.1 = ((bf16[32,128,256]{2,1,0:T(8,128)(2,1)}), bf16[32,128,256]{2,1,0:T(8,128)(2,1)}, u32[]{:S(2)}, u32[]{:S(2)}) async-start(bf16[32,128,256]{2,1,0:T(8,128)(2,1)} %bitcast.72), calls=%async_computation.1 | async-start | bytes 4194304 | tf_op jit(solution)/shard_map/all_to_all | solution.py:53
Sparse Core Ops, SparseCore 0:
  9.8 67.0 all-gather.1
where the time goes:
time: 318 us; the launch traced here: 317 us
  waiting for transfers between devices  140 us (44%)
  blocking collectives  55.2 us (17%)
  matrix products  44.7 us (14%)
  other arithmetic  26.7 us (8%)
  local copies, waits for them, and re-layouts  21.2 us (7%)
  starting transfers between devices  14.5 us (5%)
  between operations  14.3 us (4%)
    all_gather x1, waiting for transfers between devices, local(): group_q = lax.all_gather(queries, 'dev', axis=0, tiled=True)  63.8 us
    all_to_all x1, blocking collectives, from_everyone(): lax.all_to_all(jnp.broadcast_to(shard[None], (length, *shard.shape)), axi...  55.2 us
    all_to_all x1, waiting for transfers between devices, summed_on_arrival(): lax.all_to_all(pieces, axis, split_axis=0, concat_axis=0, tiled=True)  47 us
    all_to_all x1, waiting for transfers between devices, from_everyone(): lax.all_to_all(jnp.broadcast_to(shard[None], (length, *shard.shape)), axi...  28.3 us
    dot_general x16, matrix products, logits(): jnp.dot(q_block, candidates.T, preferred_element_type=jnp.float32)  24.2 us
    dot_general x8, matrix products, backward(): jnp.einsum('rc,rd->cd', logit_grad, q_block, preferred_element_type=jnp.f...  11.8 us
    sub x16, other arithmetic, positives(): targets = first_row + jnp.arange(block_rows, dtype=jnp.int32) - own_start  10.4 us
    dynamic_slice x16, local copies, waits for them, and re-layouts, local(): maxima, totals, matched = lax.map(forward, (blocks, starts))  9.35 us
  transfers between devices with their start and end apart: 3, of which 3 were waited for; matrix products, arithmetic and copies ran while one was open for 3% of the time, Pallas kernels for 0%

commit v1 on v0

--- a/solution.py
+++ b/solution.py
@@ -94,7 +94,9 @@
     own_start = dev_index * own_rows
     own_ids = lax.dynamic_slice_in_dim(item_ids, own_start, own_rows, 0)
     own_offsets = jnp.take(logq_table, own_ids, axis=0)
-    group_q = lax.all_gather(queries, "dev", axis=0, tiled=True)
+    group_q = jnp.concatenate(
+        lax.all_to_all(jnp.stack([queries] * lax.axis_size("dev")), "dev", 0, 0), axis=0
+    )
     all_rows = group_q.shape[0]
     block_rows, block_count = block_shape(all_rows)
     blocks = group_q.reshape(block_count, block_rows, feat_width)

time: 318 us -> 328 us (1.031)
  local copies, waits for them, and re-layouts: 21.2 us -> 61.3 us
  waiting for transfers between devices: 140 us -> 121 us
  between operations: 14.3 us -> 0.98 us
  starting transfers between devices: 14.5 us -> 22.6 us
  matrix products: 44.7 us -> 37 us
    all_gather x1 -> x0, waiting for transfers between devices: 63.8 us -> none  [local(): group_q = lax.all_gather(queries, 'dev', axis=0, tiled=True)]
    all_to_all x0 -> x1, waiting for transfers between devices: none -> 45.8 us  [local(): lax.all_to_all(jnp.stack([queries] * lax.axis_size('dev')), 'dev', 0, 0)]
    dynamic_update_slice x24, local copies, waits for them, and re-layouts: 1.45 us -> 32 us  [local(): maxima, totals, matched = lax.map(forward, (blocks, starts))]
    all_to_all x0 -> x1, starting transfers between devices: none -> 10.5 us  [local(): lax.all_to_all(jnp.stack([queries] * lax.axis_size('dev')), 'dev', 0, 0)]
    dot_general x16, matrix products: 24.2 us -> 16.6 us  [logits(): jnp.dot(q_block, candidates.T, preferred_element_type=jnp.float32)]
    dynamic_slice x16, local copies, waits for them, and re-layouts: 9.35 us -> 14.3 us  [local(): maxima, totals, matched = lax.map(forward, (blocks, starts))]
where the time goes in v1:
time: 328 us; the launch traced here: 325 us
  waiting for transfers between devices  121 us (37%)
  local copies, waits for them, and re-layouts  61.3 us (19%)
  blocking collectives  55.4 us (17%)
  matrix products  37 us (11%)
  other arithmetic  26.6 us (8%)
  starting transfers between devices  22.6 us (7%)
    all_to_all x1, blocking collectives, from_everyone(): lax.all_to_all(jnp.broadcast_to(shard[None], (length, *shard.shape)), axi...  55.4 us
    all_to_all x1, waiting for transfers between devices, summed_on_arrival(): lax.all_to_all(pieces, axis, split_axis=0, concat_axis=0, tiled=True)  47 us
    all_to_all x1, waiting for transfers between devices, local(): lax.all_to_all(jnp.stack([queries] * lax.axis_size('dev')), 'dev', 0, 0)  45.8 us
    dynamic_update_slice x24, local copies, waits for them, and re-layouts, local(): maxima, totals, matched = lax.map(forward, (blocks, starts))  32 us
    all_to_all x1, waiting for transfers between devices, from_everyone(): lax.all_to_all(jnp.broadcast_to(shard[None], (length, *shard.shape)), axi...  28.3 us
    dot_general x16, matrix products, logits(): jnp.dot(q_block, candidates.T, preferred_element_type=jnp.float32)  16.6 us
    dynamic_slice x16, local copies, waits for them, and re-layouts, local(): maxima, totals, matched = lax.map(forward, (blocks, starts))  14.3 us
    dot_general x8, matrix products, backward(): jnp.einsum('rc,rd->cd', logit_grad, q_block, preferred_element_type=jnp.f...  11.8 us
  transfers between devices with their start and end apart: 3, of which 3 were waited for; matrix products, arithmetic and copies ran while one was open for 3% of the time, Pallas kernels for 0%

profile of v1, /device:TPU:9, one launch (start us, length us, event | category | flops | bytes accessed | tf_op | source)
XLA Modules:
  0.0 325.3 jit_solution(136932964300004015)
XLA Ops:
  0.6 2.5 stack.2
  3.2 10.5 %all-to-all-start = ((bf16[32,128,256]{2,1,0:T(8,128)(2,1)}), bf16[32,128,256]{2,1,0:T(8,128)(2,1)S(1)}, u32[]{:S(2)}, u32[]{:S(2)}) async-start(bf16[32,128,256]{2,1,0:T(8,128)(2,1)} %stack.2), calls=%async_computation | async-start | bytes 4194304 | tf_op jit(solution)/shard_map/all_to_all | solution.py:98
  17.9 45.8 %all-to-all-done = bf16[32,128,256]{2,1,0:T(8,128)(2,1)S(1)} async-done(((bf16[32,128,256]{2,1,0:T(8,128)(2,1)}), bf16[32,128,256]{2,1,0:T(8,128)(2,1)S(1)}, u32[]{:S(2)}, u32[]{:S(2)}) %all-to-all-start) | async-done | bytes 2097184 | tf_op jit(solution)/shard_map/all_to_all | solution.py:98
  63.8 56.4 %while.30 = (s32[]{:T(128)}, f32[8,512]{1,0:T(8,128)}, f32[8,512]{1,0:T(8,128)}, f32[8,512]{1,0:T(8,128)}, bf16[8,512,256]{2,1,0:T(8,128)(2,1)S(1)}, /*index=5*/...) while((s32[]{:T(128)}, f32[8,512]{1,0:T(8,128)}, ...), condition=%wide.region_4.5_spmd.clone.clone, body=%wide.region_0.4_spmd.clone.clone.sunk | while | flops 170721408 | bytes 3241369 | solution.py:118
  123.1 4.9 %all-to-all-start.1 = ((f32[32,2,4096]{2,1,0:T(2,128)}), f32[32,2,4096]{2,1,0:T(2,128)}, u32[]{:S(2)}, u32[]{:S(2)}) async-start(f32[32,2,4096]{2,1,0:T(2,128)} %broadcast_in_dim.56), calls=%async_computation.1 | async-start | bytes 2097152 | tf_op jit(solution)/shard_map/all_to_all | solution.py:11
  128.1 28.3 %all-to-all-done.1 = f32[32,2,4096]{2,1,0:T(2,128)} async-done(((f32[32,2,4096]{2,1,0:T(2,128)}), f32[32,2,4096]{2,1,0:T(2,128)}, u32[]{:S(2)}, u32[]{:S(2)}) %all-to-all-start.1) | async-done | bytes 1048608 | tf_op jit(solution)/shard_map/all_to_all | solution.py:11
  156.4 2.7 fusion.27
  164.8 43.4 %while.31 = (s32[]{:T(128)}, f32[640,256]{1,0:T(8,128)S(1)}, bf16[8,512,256]{2,1,0:T(8,128)(2,1)}, bf16[8,512,256]{2,1,0:T(8,128)(2,1)}, bf16[640,256]{1,0:T(8,1...) while((s32[]{:T(128)}, f32[640,256]{1,0:T(8,128)S(1)}, ...), condition=%wide.region_6.7_spmd.clone.clone, body=%wide.region_5.6_spmd.clone.clone.sunk | while | flops 506594944 | bytes 4994979 | solution.py:137
  166.1 1.6 fusion.51
  171.5 1.6 fusion.51
  176.9 1.6 fusion.51
  182.4 1.6 fusion.51
  187.8 1.6 fusion.51
  189.4 1.5 convolution_add_fusion.2
  193.2 1.6 fusion.51
  194.8 1.5 convolution_add_fusion.2
  198.6 1.6 fusion.51
  204.0 1.6 fusion.51
  205.6 1.5 convolution_add_fusion.2
  208.6 55.4 %all_to_all.20 = f32[8,512,256]{2,1,0:T(8,128)} all-to-all(f32[8,512,256]{2,1,0:T(8,128)S(1)} %broadcast_in_dim.59), channel_id=1, replica_groups=mesh['grp'=8,'dev'=32] {'grp'}, dimensions={0} | all-to-all | bytes 8388608 | tf_op jit(solution)/shard_map/all_to_all | solution.py:11
  264.0 7.2 %all-to-all-start.2 = ((bf16[32,128,256]{2,1,0:T(8,128)(2,1)}), bf16[32,128,256]{2,1,0:T(8,128)(2,1)}, u32[]{:S(2)}, u32[]{:S(2)}) async-start(bf16[32,128,256]{2,1,0:T(8,128)(2,1)} %bitcast.72), calls=%async_computation.2 | async-start | bytes 4194304 | tf_op jit(solution)/shard_map/all_to_all | solution.py:53
  272.5 3.3 %reduce_sum.37 = f32[512,256]{1,0:T(8,128)} reduce(f32[8,512,256]{2,1,0:T(8,128)} %all_to_all.20, f32[]{:T(128)} %constant.43.clone.1), dimensions={0}, to_apply=%region_8.9 | reduce | flops 917504 | bytes 4718596 | tf_op jit(solution)/shard_map/reduce_sum | solution.py:58
  275.8 47.0 %all-to-all-done.2 = bf16[32,128,256]{2,1,0:T(8,128)(2,1)} async-done(((bf16[32,128,256]{2,1,0:T(8,128)(2,1)}), bf16[32,128,256]{2,1,0:T(8,128)(2,1)}, u32[]{:S(2)}, u32[]{:S(2)}) %all-to-all-start.2) | async-done | bytes 2097184 | tf_op jit(solution)/shard_map/all_to_all | solution.py:53
  322.7 2.5 convert_reduce_fusion
  (167 shorter events, 96.7 us)
Async XLA Ops:
  0.6 13.8 %copy-start = (f32[262144]{0:T(1024)S(1)}, f32[262144]{0:T(1024)}, u32[]{:S(2)}) copy-start(f32[262144]{0:T(1024)} %param.15) | copy-start | bytes 3145732
  3.1 13.8 %copy-start.4 = (f32[512]{0:T(512)S(1)}, f32[512]{0:T(512)}, u32[]{:S(2)}) copy-start(f32[512]{0:T(512)} %param.14) | copy-start | bytes 6148
  3.2 13.8 %copy-start.2 = (bf16[128,256]{1,0:T(8,128)(2,1)S(1)}, bf16[128,256]{1,0:T(8,128)(2,1)}, u32[]{:S(2)}) copy-start(bf16[128,256]{1,0:T(8,128)(2,1)} %param.11) | copy-start | bytes 196612
  3.2 60.6 %all-to-all-start = ((bf16[32,128,256]{2,1,0:T(8,128)(2,1)}), bf16[32,128,256]{2,1,0:T(8,128)(2,1)S(1)}, u32[]{:S(2)}, u32[]{:S(2)}) async-start(bf16[32,128,256]{2,1,0:T(8,128)(2,1)} %stack.2), calls=%async_computation | async-start | bytes 4194304 | tf_op jit(solution)/shard_map/all_to_all | solution.py:98
  120.2 3.0 copy-start.1
  123.1 33.2 %all-to-all-start.1 = ((f32[32,2,4096]{2,1,0:T(2,128)}), f32[32,2,4096]{2,1,0:T(2,128)}, u32[]{:S(2)}, u32[]{:S(2)}) async-start(f32[32,2,4096]{2,1,0:T(2,128)} %broadcast_in_dim.56), calls=%async_computation.1 | async-start | bytes 2097152 | tf_op jit(solution)/shard_map/all_to_all | solution.py:11
  162.3 2.5 copy-start.5
  264.0 7.2 %copy-start.3 = (f32[8,512]{1,0:T(8,128)S(1)}, f32[8,512]{1,0:T(8,128)}, u32[]{:S(2)}) copy-start(f32[8,512]{1,0:T(8,128)} %get-tuple-element.119) | copy-start | bytes 49156
  264.0 58.8 %all-to-all-start.2 = ((bf16[32,128,256]{2,1,0:T(8,128)(2,1)}), bf16[32,128,256]{2,1,0:T(8,128)(2,1)}, u32[]{:S(2)}, u32[]{:S(2)}) async-start(bf16[32,128,256]{2,1,0:T(8,128)(2,1)} %bitcast.72), calls=%async_computation.2 | async-start | bytes 4194304 | tf_op jit(solution)/shard_map/all_to_all | solution.py:53
